TPU v7x, 32 devices: a whole 2x2x4 slice. The times are simulated.
32 devices in a mesh: mem: 2 (over x), col: 16 (over z, y, core).
Axes of the slice: x: 2, y: 2, z: 4, core: 2. Of those that a mesh axis runs over, the one named last changes fastest.
Arguments:
- state_a: bfloat16 [64, 1048576], P('mem', 'col'), may hold values from -12 to 12
- state_b: bfloat16 [64, 1048576], P('mem', 'col'), may hold values from -12 to 12
- obs_index: int32 [2, 8192, 16], P(None, ('col', 'mem')), may hold values from 0 to 127
- observation_count: int32 [2, 8192], P(None, ('col', 'mem')), may hold values from 1 to 16, as said below
- obs_value: float32 [2, 8192, 16], P(None, ('col', 'mem')), may hold values from -32 to 32
- obs_weight: float32 [2, 8192, 16], P(None, ('col', 'mem')), may hold values from 0.02 to 0.2
Outputs:
- analysis_a: bfloat16 [64, 1048576], P(None, ('col', 'mem'))
- analysis_b: bfloat16 [64, 1048576], P(None, ('col', 'mem'))
- transform: float32 [64, 64], replicated
Inputs may be any that keep to these rules, and one draw needn't show every extreme that they name: Slot s of block b of group g is an observation when s < observation_count[g, b]; for each group, every aligned run of 256 blocks holds a block with all 16 slots live.
All inputs are finite; a program needn't handle non-finite values.
Results may differ from a plain program's by a relative error of at most 0.005.
Values may be sent and summed in bfloat16 or wider, within the bound.
A program may use at most 64 MiB of HBM per device.

v0:
```python
import jax
import jax.numpy as jnp
from jax import lax
from jax.sharding import PartitionSpec as P

ITERS = 24


def inverse_root(amat):
    scale = jnp.sqrt(jnp.sum(amat * amat))
    eye = jnp.eye(amat.shape[0], dtype=jnp.float32)

    def forward_step(step, carry):
        yn, zn = carry
        tm = 1.5 * eye - 0.5 * jnp.dot(zn, yn, precision=lax.Precision.HIGHEST)
        return (
            jnp.dot(yn, tm, precision=lax.Precision.HIGHEST),
            jnp.dot(tm, zn, precision=lax.Precision.HIGHEST),
        )

    yn, zn = lax.fori_loop(0, ITERS, forward_step, (amat / scale, eye))
    return (zn, scale)


def make_transform(gram_product, cross, misfit, total):
    members = gram_product.shape[0]
    scl = (members - 1.0) / total
    gs = scl * gram_product
    bs = scl * cross
    qval = scl * misfit
    tval = jnp.trace(gs)
    rho = (1.0 + qval / (members - 1.0)) / (1.0 + tval / (members - 1.0))
    amat = (members - 1.0) / rho * jnp.eye(members, dtype=jnp.float32) + gs
    zn, scale = inverse_root(amat)
    pmat = jnp.dot(zn, zn, precision=lax.Precision.HIGHEST) / scale
    wbar = jnp.dot(pmat, bs, precision=lax.Precision.HIGHEST)
    return jnp.sqrt(members - 1.0) * zn / jnp.sqrt(scale) + wbar[:, None]


def shards(state_a, state_b, obs_index, observation_count, obs_value, obs_weight):
    members = state_a.shape[0]
    group_column_sets = state_a.shape[1]
    nmem = lax.axis_size("mem")
    piece = group_column_sets // nmem
    everyone = members * nmem
    nblk = obs_index.shape[1]
    slots = obs_index.shape[2]
    width = nblk * slots
    live = (
        lax.broadcasted_iota(jnp.int32, (2, nblk, slots), 2) < observation_count[:, :, None]
    ).astype(jnp.float32)
    live = live.reshape(2, width)
    weights = live * obs_weight.reshape(2, width)
    observed = obs_value.reshape(2, width)

    def observe(columns, index, blocks):
        lanes = lax.broadcasted_iota(jnp.int32, (blocks, slots, 128), 2)
        onehot = (index[:, :, None] == lanes).astype(jnp.bfloat16)
        taken = jnp.einsum(
            "kbc,bsc->kbs",
            columns.reshape(columns.shape[0], blocks, 128),
            onehot,
            preferred_element_type=jnp.float32,
        )
        return taken.reshape(columns.shape[0], blocks * slots)

    def statistics(hx, group):
        hmean = jnp.mean(hx, axis=0)
        anomaly_rows = hx - hmean[None]
        innov = observed[group] - hmean
        wt = weights[group]
        scaled_anomaly = anomaly_rows * wt[None]
        gram_product = jnp.einsum(
            "kn,ln->kl", scaled_anomaly, anomaly_rows, precision=lax.Precision.HIGHEST
        )
        cross = jnp.einsum("kn,n->k", scaled_anomaly, innov, precision=lax.Precision.HIGHEST)
        misfit = jnp.sum(wt * innov * innov)
        extra = jnp.stack([misfit, jnp.sum(live[group])])
        return (gram_product, cross, extra)

    def regroup(state):
        return state.reshape(members, nmem, piece)

    all_index = lax.all_gather(obs_index, "mem", axis=1, tiled=True)
    local_hx = jnp.stack(
        [observe(state_a, all_index[0], nmem * nblk), observe(state_b, all_index[1], nmem * nblk)]
    ).astype(jnp.bfloat16)
    moved_hx = lax.all_to_all(
        local_hx.reshape(2, members, nmem, width), "mem", split_axis=2, concat_axis=1, tiled=True
    )
    hx_all = moved_hx.reshape(2, everyone, width).astype(jnp.float32)
    first = statistics(hx_all[0], 0)
    second = statistics(hx_all[1], 1)
    gram_product, cross, extra = lax.psum(
        (first[0] + second[0], first[1] + second[1], first[2] + second[2]), ("mem", "col")
    )
    moved_a, moved_b = (
        lax.all_to_all(regroup(state_a), "mem", split_axis=1, concat_axis=0, tiled=True),
        lax.all_to_all(regroup(state_b), "mem", split_axis=1, concat_axis=0, tiled=True),
    )
    columns = [moved_a.reshape(everyone, piece), moved_b.reshape(everyone, piece)]
    misfit = extra[0]
    total = extra[1]
    transform = make_transform(gram_product, cross, misfit, total)
    wb = transform.astype(jnp.bfloat16)
    column_total = jnp.sum(wb.astype(jnp.float32), axis=0)
    ones = jnp.ones((everyone,), jnp.bfloat16)

    def analyse(cols):
        xmean = jnp.dot(ones, cols, preferred_element_type=jnp.float32) / everyone
        mixed = jnp.dot(wb.T, cols, preferred_element_type=jnp.float32)
        return (mixed + xmean[None, :] * (1.0 - column_total)[:, None]).astype(jnp.bfloat16)

    return (analyse(columns[0]), analyse(columns[1]), transform)


def solution(mesh):
    return jax.shard_map(
        shards,
        mesh=mesh,
        in_specs=(
            P("mem", "col"),
            P("mem", "col"),
            P(None, ("col", "mem"), None),
            P(None, ("col", "mem")),
            P(None, ("col", "mem"), None),
            P(None, ("col", "mem"), None),
        ),
        out_specs=(P(None, ("col", "mem")), P(None, ("col", "mem")), P()),
        check_vma=False,
    )
```

profile of v0, /device:TPU:0, one launch (start us, length us, event | category | flops | bytes accessed | tf_op | source)
XLA Modules:
  0.0 192.1 jit_solution(10022677384199641888)
XLA Ops:
  0.6 5.8 %all_gather.3 = s32[2,512,16]{1,2,0:T(8,128)S(1)} all-gather(s32[2,256,16]{1,2,0:T(8,128)} %param.10), channel_id=1, replica_groups=mesh['mem'=2,'col'=16] {'mem'}, dimensions={1}, use_global_device_ids=true | all-gather | bytes 98304 | tf_op jit(solution)/shard_map/all_gather | solution.py:84
  6.7 4.6 %fusion.16 = bf16[512,16,32]{2,1,0:T(8,128)(2,1)S(1)} fusion(s32[512,16]{1,0:T(8,128)S(1)} %copy.40, bf16[32,65536]{1,0:T(8,128)(2,1)} %param.9), kind=kOutput, calls=%fused_computation.23 | convolution fusion | flops 68419584 | bytes 4751360 | tf_op jit(solution)/shard_map/kbc,bsc->kbs/dot_general | solution.py:59
  11.3 0.8 copy.43
  12.1 4.6 %fusion.13 = bf16[512,16,32]{2,1,0:T(8,128)(2,1)S(1)} fusion(s32[512,16]{1,0:T(8,128)S(1)} %copy.38, bf16[32,65536]{1,0:T(8,128)(2,1)} %param.8), kind=kOutput, calls=%fused_computation.22 | convolution fusion | flops 68419584 | bytes 4751360 | tf_op jit(solution)/shard_map/kbc,bsc->kbs/dot_general | solution.py:59
  16.7 0.8 copy.42
  17.5 1.1 pad_maximum_fusion
  18.6 3.6 %all-to-all-start = ((bf16[2,32,2,4096]{3,1,0,2:T(8,128)(2,1)}), bf16[2,32,2,4096]{3,1,0,2:T(8,128)(2,1)S(1)}, u32[]{:S(2)}, u32[]{:S(2)}) async-start(bf16[2,32,2,4096]{3,1,0,2:T(8,128)(2,1)} %pad_maximum_fusion), calls=%async_computation | async-start | bytes 2097152 | tf_op jit(solution)/shard_map/all_to_all | solution.py:88
  23.2 0.7 slice_reduce_fusion
  24.2 4.6 %copy.70 = bf16[4,2,8,32768]{3,2,0,1:T(8,128)(2,1)} copy(bf16[4,2,8,32768]{3,2,1,0:T(8,128)(2,1)} %bitcast.125) | data formatting | bytes 8388608 | tf_op jit(solution)/shard_map/reshape | solution.py:82
  28.8 2.3 %copy.71 = bf16[4,2,8,32768]{3,2,0,1:T(8,128)(2,1)} copy(bf16[4,2,8,32768]{3,2,1,0:T(8,128)(2,1)S(1)} %bitcast.126) | data formatting | bytes 8388608 | tf_op jit(solution)/shard_map/reshape | solution.py:82
  31.2 4.0 %all-to-all-done = bf16[2,32,2,4096]{3,1,0,2:T(8,128)(2,1)S(1)} async-done(((bf16[2,32,2,4096]{3,1,0,2:T(8,128)(2,1)}), bf16[2,32,2,4096]{3,1,0,2:T(8,128)(2,1)S(1)}, u32[]{:S(2)}, u32[]{:S(2)}) %all-to-all-start) | async-done | bytes 1048608 | tf_op jit(solution)/shard_map/all_to_all | solution.py:88
  35.1 5.6 %all-to-all-start.2 = ((bf16[32,2,32768]{2,0,1:T(8,128)(2,1)}), bf16[32,2,32768]{2,0,1:T(8,128)(2,1)}, u32[]{:S(2)}, u32[]{:S(2)}) async-start(bf16[32,2,32768]{2,0,1:T(8,128)(2,1)} %bitcast.124), calls=%async_computation.2 | async-start | bytes 8388608 | tf_op jit(solution)/shard_map/all_to_all | solution.py:99
  41.0 0.3 slice_reduce_fusion.2
  41.3 0.6 fusion.38
  42.1 0.7 fusion.39
  43.0 2.6 %maximum_add_fusion = f32[2]{0:T(128)S(1)} fusion(f32[1]{0:T(128)} %bitcast.10, f32[1]{0:T(128)} %bitcast.9, f32[1]{0:T(128)} %bitcast.14, f32[1]{0:T(128)} %bitcast.13), kind=kLoop, calls=%fused_computation.71 | loop fusion | flops 6 | bytes 24 | tf_op jit(solution)/shard_map/add | solution.py:95
  45.8 0.9 convolution_bitcast_fusion.1
  46.7 1.0 fusion.19
  47.7 1.0 fusion.25
  48.7 1.0 convolution_add_fusion.2
  49.7 71.5 %all-reduce = (f32[64,64]{1,0:T(8,128)S(1)}, f32[2]{0:T(128)S(1)}, f32[64]{0:T(128)S(1)}) all-reduce(f32[64,64]{1,0:T(8,128)S(1)} %convolution_add_fusion.2, f32[2]{0:T(128)S(1)} %maximum_add_fusion, f32[64]{0:T(128)S(1)} %fusion.19), channel_id=1, replica_groups=mesh['mem'=2,'col'=16] {'mem','col'}, use_global_device_ids=true, to_apply=%region_7.0 | all-reduce | flops 4162 | bytes 33296 | tf_op jit(solution)/shard_map/psum | solution.py:94
  121.2 0.6 fusion.53
  123.1 0.6 select_reduce_fusion
  124.4 0.6 multiply_reduce_fusion
  125.8 5.8 %all-to-all-start.1 = ((bf16[32,2,32768]{2,0,1:T(8,128)(2,1)}), bf16[32,2,32768]{2,0,1:T(8,128)(2,1)}, u32[]{:S(2)}, u32[]{:S(2)}) async-start(bf16[32,2,32768]{2,0,1:T(8,128)(2,1)} %bitcast.123), calls=%async_computation.1 | async-start | bytes 8388608 | tf_op jit(solution)/shard_map/all_to_all | solution.py:98
  131.6 15.5 %while.13 = (s32[]{:T(128)}, f32[64,64]{0,1:T(8,128)S(1)}, f32[64,64]{1,0:T(8,128)S(1)}, s32[]{:T(128)}) while((s32[]{:T(128)}, f32[64,64]{0,1:T(8,128)S(1)}, f32[64,64]{1,0:T(8,128)S(1)}, s32[]{:T(128)}) %tuple.41), condition=%wide.region_11.12_spmd.clone, body=%wide.region_10.11_spmd.clone.sunk | while | flops 9453570 | bytes 213045 | solution.py:21
  132.0 0.2 convolution_bitcast_fusion.5
  132.6 0.2 convolution_bitcast_fusion.5
  133.3 0.2 convolution_bitcast_fusion.5
  133.9 0.2 convolution_bitcast_fusion.5
  134.5 0.2 convolution_bitcast_fusion.5
  135.2 0.2 convolution_bitcast_fusion.5
  135.8 0.2 convolution_bitcast_fusion.5
  136.5 0.2 convolution_bitcast_fusion.5
  137.1 0.2 convolution_bitcast_fusion.5
  137.8 0.2 convolution_bitcast_fusion.5
  138.4 0.2 convolution_bitcast_fusion.5
  139.0 0.2 convolution_bitcast_fusion.5
  139.7 0.2 convolution_bitcast_fusion.5
  140.3 0.2 convolution_bitcast_fusion.5
  144.2 0.2 convolution_bitcast_fusion.5
  145.5 0.2 convolution_bitcast_fusion.5
  146.8 0.2 convolution_bitcast_fusion.5
  147.5 2.8 %fusion.42 = f32[1,32768]{1,0:T(1,128)S(1)} fusion(bf16[64,32768]{1,0:T(8,128)(2,1)} %bitcast.35), kind=kOutput, calls=%fused_computation.74 | convolution fusion | flops 4194304 | bytes 4325376 | tf_op jit(solution)/shard_map/dot_general | solution.py:110
  150.4 27.9 %all-to-all-done.1 = bf16[32,2,32768]{2,0,1:T(8,128)(2,1)} async-done(((bf16[32,2,32768]{2,0,1:T(8,128)(2,1)}), bf16[32,2,32768]{2,0,1:T(8,128)(2,1)}, u32[]{:S(2)}, u32[]{:S(2)}) %all-to-all-start.1) | async-done | bytes 4194336 | tf_op jit(solution)/shard_map/all_to_all | solution.py:98
  178.3 2.8 %fusion.44 = f32[1,32768]{1,0:T(1,128)S(1)} fusion(bf16[64,32768]{1,0:T(8,128)(2,1)} %bitcast.29), kind=kOutput, calls=%fused_computation.76 | convolution fusion | flops 4194304 | bytes 4325376 | tf_op jit(solution)/shard_map/dot_general | solution.py:110
  181.1 5.5 %fusion.4 = bf16[64,32768]{1,0:T(8,128)(2,1)} fusion(bf16[64,32768]{1,0:T(8,128)(2,1)} %bitcast.35, f32[32768]{0:T(1024)S(1)} %broadcast_multiply_fusion, f32[64]{0:T(128)S(1)} %broadcast_subtract_fusion, f32[64,64]{1,0:T(8,128)S(1)} %get-tuple-element.60), kind=kOutput, calls=%fused_computation.8 | convolution fusion | flops 274731008 | bytes 8536320 | tf_op jit(solution)/shard_map/dot_general | solution.py:111
  186.6 5.5 %fusion.3 = bf16[64,32768]{1,0:T(8,128)(2,1)} fusion(bf16[64,32768]{1,0:T(8,128)(2,1)} %bitcast.29, f32[64]{0:T(128)S(1)} %broadcast_subtract_fusion, f32[32768]{0:T(1024)S(1)} %broadcast_multiply_fusion.1, f32[64,64]{1,0:T(8,128)S(1)} %get-tuple-element.60), kind=kOutput, calls=%fused_computation.7 | convolution fusion | flops 274731008 | bytes 8536320 | tf_op jit(solution)/shard_map/dot_general | solution.py:111
  (148 shorter events, 13.1 us)
Async XLA Ops:
  16.6 5.5 %copy-start.3 = (f32[2,256,16]{1,2,0:T(8,128)S(1)}, f32[2,256,16]{1,2,0:T(8,128)}, u32[]{:S(2)}) copy-start(f32[2,256,16]{1,2,0:T(8,128)} %param.12) | copy-start | bytes 98308
  16.7 6.1 %copy-start.2 = (f32[2,256,16]{1,2,0:T(8,128)S(1)}, f32[2,256,16]{1,2,0:T(8,128)}, u32[]{:S(2)}) copy-start(f32[2,256,16]{1,2,0:T(8,128)} %param.13) | copy-start | bytes 98308
  16.7 6.4 %copy-start.4 = (s32[2,256]{1,0:T(2,128)S(1)}, s32[2,256]{1,0:T(2,128)}, u32[]{:S(2)}) copy-start(s32[2,256]{1,0:T(2,128)} %param.11) | copy-start | bytes 6148
  18.6 16.6 %all-to-all-start = ((bf16[2,32,2,4096]{3,1,0,2:T(8,128)(2,1)}), bf16[2,32,2,4096]{3,1,0,2:T(8,128)(2,1)S(1)}, u32[]{:S(2)}, u32[]{:S(2)}) async-start(bf16[2,32,2,4096]{3,1,0,2:T(8,128)(2,1)} %pad_maximum_fusion), calls=%async_computation | async-start | bytes 2097152 | tf_op jit(solution)/shard_map/all_to_all | solution.py:88
  24.1 4.6 %copy-start = (bf16[32,65536]{1,0:T(8,128)(2,1)S(1)}, bf16[32,65536]{1,0:T(8,128)(2,1)}, u32[]{:S(2)}) copy-start(bf16[32,65536]{1,0:T(8,128)(2,1)} %param.8) | copy-start | bytes 12582916
  35.1 90.6 %all-to-all-start.2 = ((bf16[32,2,32768]{2,0,1:T(8,128)(2,1)}), bf16[32,2,32768]{2,0,1:T(8,128)(2,1)}, u32[]{:S(2)}, u32[]{:S(2)}) async-start(bf16[32,2,32768]{2,0,1:T(8,128)(2,1)} %bitcast.124), calls=%async_computation.2 | async-start | bytes 8388608 | tf_op jit(solution)/shard_map/all_to_all | solution.py:99
  125.8 52.5 %all-to-all-start.1 = ((bf16[32,2,32768]{2,0,1:T(8,128)(2,1)}), bf16[32,2,32768]{2,0,1:T(8,128)(2,1)}, u32[]{:S(2)}, u32[]{:S(2)}) async-start(bf16[32,2,32768]{2,0,1:T(8,128)(2,1)} %bitcast.123), calls=%async_computation.1 | async-start | bytes 8388608 | tf_op jit(solution)/shard_map/all_to_all | solution.py:98
  147.5 39.1 %copy-start.1 = (f32[64,64]{1,0:T(8,128)}, f32[64,64]{1,0:T(8,128)S(1)}, u32[]{:S(2)}) copy-start(f32[64,64]{1,0:T(8,128)S(1)} %get-tuple-element.60) | copy-start | bytes 49156
where the time goes:
time: 193 us; the launch traced here: 192 us
  blocking collectives  77.2 us (40%)
  matrix products  44 us (23%)
  waiting for transfers between devices  31.8 us (16%)
  starting transfers between devices  15 us (8%)
  local copies, waits for them, and re-layouts  11.2 us (6%)
  other arithmetic  7.89 us (4%)
  between operations  3.67 us (2%)
    psum x1, blocking collectives, shards(): lax.psum((first[0] + second[0], first[1] + second[1], first[2] + second[2...  71.5 us
    all_to_all x1, waiting for transfers between devices, shards(): lax.all_to_all(regroup(state_a), 'mem', split_axis=1, concat_axis=0, tile...  27.9 us
    dot_general x2, matrix products, analyse(): mixed = jnp.dot(wb.T, cols, preferred_element_type=jnp.float32)  11 us
    dot_general x2, matrix products, observe(): jnp.einsum('kbc,bsc->kbs', columns.reshape(columns.shape[0], blocks, 128)...  9.13 us
    reshape x2, local copies, waits for them, and re-layouts, regroup(): return state.reshape(members, nmem, piece)  6.94 us
    all_gather x1, blocking collectives, shards(): all_index = lax.all_gather(obs_index, 'mem', axis=1, tiled=True)  5.79 us
    all_to_all x1, starting transfers between devices, shards(): lax.all_to_all(regroup(state_a), 'mem', split_axis=1, concat_axis=0, tile...  5.79 us
    dot_general x2, matrix products, analyse(): xmean = jnp.dot(ones, cols, preferred_element_type=jnp.float32) / everyone  5.68 us
  transfers between devices with their start and end apart: 3, of which 2 were waited for; matrix products, arithmetic and copies ran while one was open for 19% of the time, Pallas kernels for 0%

commit v1 on v0

v1 whole, which is shorter than its diff:
```python
import functools

import jax
import jax.numpy as jnp
from jax import lax
from jax.experimental import pallas as pl
from jax.experimental.pallas import tpu as pltpu
from jax.sharding import PartitionSpec as P

ITERS = 24
LANES = 128
HIGH = lax.Precision.HIGHEST
MESH = pl.DeviceIdType.MESH
ROWS = 128
CHUNK = 2048
FIRST_PART = 0.34
HX_CUTS = 4


def bits(n):
    return [1 << i for i in range(n.bit_length() - 1)]


def transform_of(gram, members):
    members = members
    g = gram[:members, :members]
    cross = gram[members : members + 1, :members]
    misfit = gram[members : members + 1, members : members + 1]
    total = gram[members + 1 : members + 2, members + 1 : members + 2]
    rows = lax.broadcasted_iota(jnp.int32, (members, members), 0)
    cols = lax.broadcasted_iota(jnp.int32, (members, members), 1)
    eye = (rows == cols).astype(jnp.float32)

    def whole(x):
        return jnp.sum(jnp.sum(x, axis=1, keepdims=True), axis=0, keepdims=True)

    def parts(x):
        hi = x.astype(jnp.bfloat16)
        rest = x - hi.astype(jnp.float32)
        mid = rest.astype(jnp.bfloat16)
        low = (rest - mid.astype(jnp.float32)).astype(jnp.bfloat16)
        return hi, mid, low

    def dot(a, b):
        total = None
        for i in range(3):
            left = jnp.concatenate(a[: 3 - i], axis=0) if i < 2 else a[0]
            out = jnp.dot(left, b[i], preferred_element_type=jnp.float32)
            for j in reversed(range(3 - i)):
                block = out[j * members : (j + 1) * members]
                total = block if total is None else total + block
        return total

    dof = members - 1.0
    scl = dof / total
    gs = scl * g
    bs = scl * cross
    rho = (1.0 + scl * misfit / dof) / (1.0 + whole(gs * eye) / dof)
    amat = dof / rho * eye + gs
    scale = jnp.sqrt(whole(amat * amat))

    def step(_, carry):
        yn, zn = carry
        yp, zp = parts(yn), parts(zn)
        tp = parts(1.5 * eye - 0.5 * dot(zp, yp))
        return dot(yp, tp), dot(tp, zp)

    _, zn = lax.fori_loop(0, ITERS, step, (amat / scale, eye))
    zp = parts(zn)
    wbar = jnp.sum(dot(zp, zp) / scale * bs, axis=1, keepdims=True)
    return jnp.sqrt(dof) * zn / jnp.sqrt(scale) + wbar


def exchange_kernel(
    nmem, ncol, sa, sb, idx, val, wgt, cnt, ra, rb, tr,
    st, idx_in, hx, cur, got, load_sem, own_sem, idx_s, idx_r, hx_s, hx_r, st_s, st_r, red_s, red_r,
):
    me = lax.axis_index("mem")
    col = lax.axis_index("col")
    mk = sa.shape[0]
    members = mk * nmem
    piece = sa.shape[1] // nmem
    width = idx.shape[1]
    half = width // 2
    states, received = (sa, sb), (ra, rb)
    chunk = min(CHUNK, piece)
    cuts = piece // chunk
    peers = [lax.rem(me + d, nmem) for d in range(1, nmem)]
    across = [{"mem": me ^ b} for b in bits(nmem)] + [{"col": col ^ b} for b in bits(ncol)]
    col_peers = [col ^ b for b in bits(ncol)]

    def cols_of(owner, start, size):
        return pl.ds(pl.multiple_of(owner * piece + start, LANES), size)

    my_rows = pl.ds(pl.multiple_of(me * mk, mk), mk)

    loads = []
    for d in range(nmem):
        owner = peers[d - 1] if d else me
        for g in range(2):
            loads.append(
                pltpu.make_async_copy(
                    states[g].at[:, cols_of(owner, 0, piece)],
                    st.at[g, :, cols_of(owner, 0, piece)],
                    load_sem.at[d, g],
                )
            )
            loads[-1].start()

    barrier = pltpu.get_barrier_semaphore()
    for p in peers:
        pl.semaphore_signal(barrier, inc=1, device_id={"mem": p}, device_id_type=MESH)
    for c in col_peers:
        pl.semaphore_signal(barrier, inc=1, device_id={"col": c}, device_id_type=MESH)
    pl.semaphore_wait(barrier, len(peers) + len(col_peers))

    index_copies = []
    for d, p in enumerate(peers):
        index_copies.append(
            pltpu.make_async_remote_copy(
                idx, idx_in.at[d], idx_s.at[d], idx_r.at[d], device_id={"mem": p}, device_id_type=MESH
            )
        )
        index_copies[-1].start()

    moves = []
    for q in range(cuts):
        for g in range(2):
            for d, p in enumerate(peers):
                n = len(moves)
                moves.append(
                    pltpu.make_async_remote_copy(
                        states[g].at[:, cols_of(p, q * chunk, chunk)],
                        received[g].at[my_rows, pl.ds(q * chunk, chunk)],
                        st_s.at[n],
                        st_r.at[n],
                        device_id={"mem": p},
                        device_id_type=MESH,
                    )
                )
    first = int(len(moves) * FIRST_PART)
    for m in moves[:first]:
        m.start()

    def gather(index, owner, start, size, put):
        lane = lax.broadcasted_iota(jnp.int32, (mk, LANES), 1) // 16

        def row(r, _):
            at = pl.multiple_of(start + r * LANES, LANES)
            g = start // half
            base = (at - g * half) * 8
            s = st[g, :, cols_of(owner, base, 8 * LANES)].astype(jnp.float32)
            ir = jnp.broadcast_to(index[:, pl.ds(at, LANES)], (mk, LANES))
            out = jnp.zeros((mk, LANES), jnp.float32)
            for j in range(8):
                picked = jnp.take_along_axis(s[:, j * LANES : (j + 1) * LANES], ir, axis=1)
                out = jnp.where(lane == j, picked, out)
            put(pl.ds(at, LANES), out.astype(jnp.bfloat16))
            return 0

        lax.fori_loop(0, size // LANES, row, 0)

    step = width // HX_CUTS
    hx_copies = []
    for d, p in enumerate(peers):
        for g in range(2):
            loads[2 * (d + 1) + g].wait()
        index_copies[nmem - 2 - d].wait()
        for h in range(HX_CUTS):

            def put(where, value):
                hx[nmem + d, :, where] = value

            gather(idx_in.at[nmem - 2 - d], p, h * step, step, put)
            hx_copies.append(
                pltpu.make_async_remote_copy(
                    hx.at[nmem + d, :, pl.ds(h * step, step)],
                    hx.at[me, :, pl.ds(h * step, step)],
                    hx_s.at[d, h],
                    hx_r.at[d, h],
                    device_id={"mem": p},
                    device_id_type=MESH,
                )
            )
            if len(hx_copies) > 1:
                hx_copies[-2].start()
    for g in range(2):
        loads[g].wait()
    keep = []
    for g in range(2):
        keep.append(
            pltpu.make_async_copy(
                st.at[g, :, cols_of(me, 0, piece)], received[g].at[my_rows, :], own_sem.at[g]
            )
        )
        keep[-1].start()

    def put_own(where, value):
        hx[me, :, where] = value

    gather(idx, me, 0, step, put_own)
    hx_copies[-1].start()
    for h in range(1, HX_CUTS):
        gather(idx, me, h * step, step, put_own)
    for c in hx_copies:
        c.wait()

    span = min(1024, half)

    def accumulate(i, acc):
        where = pl.ds(pl.multiple_of(i * span, LANES), span)
        x = jnp.concatenate([hx[m, :, where].astype(jnp.float32) for m in range(nmem)], axis=0)
        hmean = jnp.sum(x, axis=0, keepdims=True) / members
        rest = jnp.zeros((ROWS - members - 1, span), jnp.float32)
        aug = jnp.concatenate([x - hmean, val[:, where] - hmean, rest], axis=0)
        return acc + lax.dot_general(
            aug * wgt[:, where], aug, (((1,), (1,)), ((), ())), precision=HIGH,
            preferred_element_type=jnp.float32,
        )

    gram = lax.fori_loop(0, width // span, accumulate, jnp.zeros((ROWS, ROWS), jnp.float32))
    live = cnt[...].astype(jnp.float32)
    live = jnp.sum(jnp.sum(live, axis=1, keepdims=True), axis=0, keepdims=True)
    rows = lax.broadcasted_iota(jnp.int32, (ROWS, ROWS), 0)
    cols = lax.broadcasted_iota(jnp.int32, (ROWS, ROWS), 1)
    gram = jnp.where((rows == members + 1) & (cols == members + 1), live, gram)
    cur[0] = gram
    started = len(moves) if not bits(nmem) else first
    for s, peer in enumerate(across):
        copy = pltpu.make_async_remote_copy(
            cur.at[s], got.at[s], red_s.at[s], red_r.at[s], device_id=peer, device_id_type=MESH
        )
        copy.start()
        if s + 1 == len(bits(nmem)):
            for m in moves[started:]:
                m.start()
        copy.wait()
        cur[s + 1] = cur[s] + got[s]
    tr[...] = transform_of(cur[len(across)], members)
    for c in keep:
        c.wait()
    for m in moves:
        m.wait()


def exchange(state_a, state_b, idx, val, wgt, cnt):
    nmem, ncol = lax.axis_size("mem"), lax.axis_size("col")
    mk, held = state_a.shape
    piece = held // nmem
    width = idx.shape[1]
    members = mk * nmem
    steps = len(bits(nmem)) + len(bits(ncol))
    moves = 2 * (nmem - 1) * (piece // min(CHUNK, piece))
    dma = pltpu.SemaphoreType.DMA
    hbm = pl.BlockSpec(memory_space=pl.ANY)
    vmem = pl.BlockSpec(memory_space=pltpu.VMEM)
    return pl.pallas_call(
        functools.partial(exchange_kernel, nmem, ncol),
        out_shape=(
            jax.ShapeDtypeStruct((members, piece), jnp.bfloat16),
            jax.ShapeDtypeStruct((members, piece), jnp.bfloat16),
            jax.ShapeDtypeStruct((members, members), jnp.float32),
        ),
        in_specs=[hbm, hbm, vmem, vmem, vmem, vmem],
        out_specs=(hbm, hbm, vmem),
        scratch_shapes=[
            pltpu.VMEM((2, mk, held), jnp.bfloat16),
            pltpu.VMEM((nmem - 1, 1, width), jnp.int32),
            pltpu.VMEM((2 * nmem - 1, mk, width), jnp.bfloat16),
            pltpu.VMEM((steps + 1, ROWS, LANES), jnp.float32),
            pltpu.VMEM((steps, ROWS, LANES), jnp.float32),
            dma((nmem, 2)),
            dma((2,)),
            dma((nmem - 1,)),
            dma((nmem - 1,)),
            dma((nmem - 1, HX_CUTS)),
            dma((nmem - 1, HX_CUTS)),
            dma((moves,)),
            dma((moves,)),
            dma((steps,)),
            dma((steps,)),
        ],
        compiler_params=pltpu.CompilerParams(
            collective_id=0, has_side_effects=True, vmem_limit_bytes=62 * 2**20
        ),
        name="exchange",
    )(state_a, state_b, idx, val, wgt, cnt)


def apply_kernel(tr, xa, xb, oa, ob, lhs, coef):
    members = tr.shape[0]

    @pl.when(pl.program_id(0) == 0)
    def _():
        wt = tr[...].T.astype(jnp.bfloat16)
        lhs[:members, :] = wt
        lhs[members:, :] = jnp.full((16, members), 1.0 / members, jnp.bfloat16)
        coef[...] = 1.0 - jnp.sum(wt.astype(jnp.float32), axis=1, keepdims=True)

    for x, o in ((xa, oa), (xb, ob)):
        mixed = jnp.dot(lhs[...], x[...], preferred_element_type=jnp.float32)
        xmean = mixed[members : members + 1]
        o[...] = (mixed[:members] + coef[...] * xmean).astype(o.dtype)


def apply(tr, xa, xb):
    members, piece = xa.shape
    block = min(4096, piece)
    wide = pl.BlockSpec((members, block), lambda i: (0, i))
    return pl.pallas_call(
        apply_kernel,
        grid=(piece // block,),
        out_shape=(jax.ShapeDtypeStruct(xa.shape, xa.dtype),) * 2,
        in_specs=[pl.BlockSpec((members, members), lambda i: (0, 0)), wide, wide],
        out_specs=(wide, wide),
        scratch_shapes=[
            pltpu.VMEM((members + 16, members), jnp.bfloat16),
            pltpu.VMEM((members, 1), jnp.float32),
        ],
        compiler_params=pltpu.CompilerParams(dimension_semantics=("arbitrary",)),
        name="apply",
    )(tr, xa, xb)


def shards(state_a, state_b, obs_index, observation_count, obs_value, obs_weight):
    nblk, slots = obs_index.shape[1:]
    width = 2 * nblk * slots
    live = lax.broadcasted_iota(jnp.int32, obs_weight.shape, 2) < observation_count[:, :, None]
    weights = jnp.where(live, obs_weight, 0.0).reshape(1, width)
    ra, rb, transform = exchange(
        state_a, state_b, obs_index.reshape(1, width), obs_value.reshape(1, width), weights,
        observation_count,
    )
    out_a, out_b = apply(transform, ra, rb)
    return (out_a, out_b, transform)


def solution(mesh):
    return jax.shard_map(
        shards,
        mesh=mesh,
        in_specs=(
            P("mem", "col"),
            P("mem", "col"),
            P(None, ("col", "mem"), None),
            P(None, ("col", "mem")),
            P(None, ("col", "mem"), None),
            P(None, ("col", "mem"), None),
        ),
        out_specs=(P(None, ("col", "mem")), P(None, ("col", "mem")), P()),
        check_vma=False,
    )
```

time: 193 us -> 134 us (0.69)
  Pallas kernels: 0 us -> 127 us
  blocking collectives: 77.2 us -> 0 us
  matrix products: 44 us -> 0 us
  waiting for transfers between devices: 31.8 us -> 0 us
  starting transfers between devices: 15 us -> 0 us
  other arithmetic: 7.89 us -> 0.77 us
  local copies, waits for them, and re-layouts: 11.2 us -> 4.81 us
  between operations: 3.67 us -> 0.67 us
    pallas_call x0 -> x2, Pallas kernels: none -> 127 us  [the longest x1 117 us: exchange(): pl.pallas_call(functools.partial(exchange_kernel, nmem, ncol), out_shape=...]
    psum x1 -> x0, blocking collectives: 71.5 us -> none  [shards(): lax.psum((first[0] + second[0], first[1] + second[1], first[2] + second[2...]
    dot_general x84 -> x0, matrix products: 44 us -> none  [the longest x2 11 us: analyse(): mixed = jnp.dot(wb.T, cols, preferred_element_type=jnp.float32)]
    all_to_all x3 -> x0, waiting for transfers between devices: 31.8 us -> none  [the longest x1 27.9 us: shards(): lax.all_to_all(regroup(state_a), 'mem', split_axis=1, concat_axis=0, tile...]
    all_to_all x3 -> x0, starting transfers between devices: 15 us -> none  [the longest x1 5.79 us: shards(): lax.all_to_all(regroup(state_a), 'mem', split_axis=1, concat_axis=0, tile...]
    all_gather x1 -> x0, blocking collectives: 5.79 us -> none  [shards(): all_index = lax.all_gather(obs_index, 'mem', axis=1, tiled=True)]
    reshape x3, local copies, waits for them, and re-layouts: 7.1 us -> 2.31 us  [the longest x1 0.77 us: shards(): weights = jnp.where(live, obs_weight, 0.0).reshape(1, width)]
    reduce_sum x7 -> x0, other arithmetic: 3.59 us -> none  [the longest x2 1.28 us: statistics(): misfit = jnp.sum(wt * innov * innov)]
  transfers between devices with their start and end apart: 3 -> 0, of which waited for: 2 -> 0; matrix products, arithmetic and copies ran while one was open for 19% -> 0% of each run, Pallas kernels for 0% -> 0%
where the time goes in v1:
time: 134 us; the launch traced here: 133 us
  Pallas kernels  127 us (95%)
  local copies, waits for them, and re-layouts  4.81 us (4%)
    pallas_call x1, Pallas kernels, exchange(): pl.pallas_call(functools.partial(exchange_kernel, nmem, ncol), out_shape=...  117 us
    pallas_call x1, Pallas kernels, apply(): pl.pallas_call(apply_kernel, grid=(piece // block,), out_shape=(jax.Shape...  10.2 us

profile of v1, /device:TPU:0, one launch (start us, length us, event | category | flops | bytes accessed | tf_op | source)
XLA Modules:
  0.0 133.3 jit_solution(8719758912012272181)
XLA Ops:
  0.6 0.8 fusion
  1.4 0.1 copy.14
  1.5 0.8 reshape.18.wgt
  2.3 0.9 copy.12
  3.2 0.8 reshape.16.idx
  4.0 0.9 copy.13
  4.8 0.8 reshape.17.val
  5.6 116.8 %exchange.1 = (bf16[64,32768]{1,0:T(8,128)(2,1)}, bf16[64,32768]{1,0:T(8,128)(2,1)}, f32[64,64]{1,0:T(8,128)}) custom-call(bf16[32,65536]{1,0:T(8,128)(2,1)} %sa.1, bf16[32,65536]{1,0:T(8,128)(2,1)} %sb.1, s32[1,8192]{1,0:T(1,128)} %reshape.16.idx, f32[1,8192]{1,0:T(1,128)} %reshape.17.val, f32[1,8192]{1,0:T(1,128)} %reshape.18.wgt, s32[2,256]{1,0:T(2,128)} %cnt.1), custom_call_target="tpu_custom_call" | custom-call | tf_op jit(solution)/shard_map/exchange/pallas_call | solution.py:257
  122.4 0.0 copy-start
  122.4 10.2 %apply.1 = (bf16[64,32768]{1,0:T(8,128)(2,1)}, bf16[64,32768]{1,0:T(8,128)(2,1)}) custom-call(f32[64,64]{1,0:T(8,128)} %get-tuple-element.18.tr, bf16[64,32768]{1,0:T(8,128)(2,1)} %get-tuple-element.9.xa, bf16[64,32768]{1,0:T(8,128)(2,1)} %get-tuple-element.10.xb), custom_call_target="tpu_custom_call" | custom-call | tf_op jit(solution)/shard_map/apply/pallas_call | solution.py:310
  132.7 0.0 copy-done
  132.7 0.6 copy.16
Async XLA Ops:
  122.4 10.2 %copy-start = (f32[64,64]{1,0:T(8,128)S(1)}, f32[64,64]{1,0:T(8,128)}, u32[]{:S(2)}) copy-start(f32[64,64]{1,0:T(8,128)} %get-tuple-element.18.tr) | copy-start | bytes 49156
